TPU v7x, 256 devices: a whole 4x4x8 slice. The times are simulated.
256 devices in a mesh: cols: 64 (over y, z, x_lo), walk: 4 (over x_hi, core).
Axes of the slice: x: 4 (x_hi: 2, x_lo: 2; x = x_hi * 2 + x_lo), y: 4, z: 8, core: 2. Of those that a mesh axis runs over, the one named last changes fastest.
Arguments:
- green_by_column: float32 [4, 4096, 4096], P('walk', 'cols'), parts along dimension 0, may hold values from -1.5 to 1.5
- field: int32 [4, 3, 4096], P('walk'), parts along dimension 0, may hold values from 0 to 1
Outputs:
- wrapped: float32 [4, 4096, 4096], P('walk', 'cols'), parts along dimension 0
There are 4 independent parts, one for each index of `walk`. A program takes and returns all parts, laid end to end along the dimension named above; each array names one. Nothing has to cross between parts.
All inputs are finite; a program needn't handle non-finite values.
Results may differ from a plain program's by a relative error of at most 0.00012.
Values sent between devices are 32-bit elements; how exact they have to be, the bound alone decides.
A program may use at most 64 MiB of HBM per device.

v0:
```python
import jax
import jax.numpy as jnp
import numpy as np
from jax import lax
from jax.experimental import pallas as pl
from jax.experimental.pallas import tpu as pltpu
from jax.sharding import PartitionSpec as P

L = 64
SITES = L * L
SLICES = 3
PEERS = 64
HALF = 32
CHUNKS = 4
PER_CHUNK = HALF // CHUNKS
PITCH_IN = 72
PITCH_OUT = 40
PITCH_X = 72

hop_rate = 0.6
coupling = 0.65373
UP = float(np.exp(coupling))
DOWN = float(np.exp(-coupling))

MESH = pl.DeviceIdType.MESH


def circulant(rate):
    k = np.arange(L)
    spectrum = np.exp(rate * np.cos(2.0 * np.pi * k / L))
    differ = k[:, None] - k[None, :]
    waves = np.cos(2.0 * np.pi * (differ[:, :, None] * k) / L)
    return (waves * spectrum).sum(-1) / L


def high_low(matrix):
    matrix = matrix.astype(np.float32)
    high = matrix.astype(jnp.bfloat16)
    low = (matrix - high.astype(np.float32)).astype(jnp.bfloat16)
    return high, low


def as_left(matrix):
    high, low = high_low(matrix)
    return np.concatenate([high, low, high], axis=1)


def as_right(matrix):
    both = np.kron(np.eye(2), matrix)
    high, low = high_low(both)
    upper = np.concatenate([high, low], axis=1)
    lower = np.concatenate([high, np.zeros_like(low)], axis=1)
    return np.concatenate([upper, lower], axis=0)


def split(values):
    high = values.astype(jnp.bfloat16)
    low = (values - high.astype(jnp.float32)).astype(jnp.bfloat16)
    return high, low


def mix_rows(weights, values):
    high, low = split(values)
    stacked = jnp.concatenate([high, high, low], axis=0)
    return jnp.dot(weights, stacked, preferred_element_type=jnp.float32)


def mix_lanes(values, weights):
    high, low = split(values)
    wide = jnp.concatenate([high, low], axis=1)
    both = jnp.dot(wide, weights, preferred_element_type=jnp.float32)
    return both[:, :128] + both[:, 128:]


def lane(shape):
    return lax.broadcasted_iota(jnp.int32, shape, len(shape) - 1)


def swap_halves(first, second):
    low = lane(first.shape) < 64
    return (
        jnp.where(low, first, pltpu.roll(second, 64, 1)),
        jnp.where(low, pltpu.roll(first, 64, 1), second),
    )


def rows_of_pair(pair):
    first, second = swap_halves(*pair)
    return jnp.concatenate([first, second], axis=0)


def pair_of_rows(rows):
    return swap_halves(rows[:HALF], rows[HALF:])


def beside(tiles):
    return jnp.concatenate(tiles, axis=1)


def kernel(
    green_ref, field_ref, left_ref, last_ref, lanes_ref, right_ref, out_ref,
    held, flags, gain, turn, own_scale, scale_x, scale_y,
    outgoing, arrived, lines, returning, landed,
    load_sems, send_sem, recv_sems, back_send_sem, back_recv_sems,
):
    me = lax.axis_index("cols")
    barrier = pltpu.get_barrier_semaphore()

    loads = [
        pltpu.make_async_copy(
            green_ref.at[:, pl.ds(t * 128, 128)],
            held.at[pl.ds(t * PITCH_IN, L), :],
            load_sems.at[t],
        )
        for t in range(HALF)
    ]
    for load in loads:
        load.start()

    def greet(k, carry):
        pl.semaphore_signal(
            barrier, inc=1, device_id={"cols": lax.rem(me + k, PEERS)}, device_id_type=MESH
        )
        return carry

    lax.fori_loop(1, PEERS, greet, 0)

    for t in range(HALF):
        flags[pl.ds(t, SLICES, stride=HALF), :] = field_ref[:, t * 128 : (t + 1) * 128].astype(jnp.float32)
    low_half = lane((HALF, 128)) < 64
    for moment in range(SLICES):
        bits = flags[moment * HALF : (moment + 1) * HALF, :]
        turned = pltpu.roll(bits, 64, 1)
        even = jnp.where(low_half, bits, turned)
        odd = jnp.where(low_half, turned, bits)
        gain[moment * L : moment * L + HALF, :] = jnp.where(even > 0.5, UP, DOWN)
        gain[moment * L + HALF : (moment + 1) * L, :] = jnp.where(odd > 0.5, UP, DOWN)
        turn[pl.ds(moment * L, HALF, stride=2), :] = bits
        turn[pl.ds(moment * L + 1, HALF, stride=2), :] = turned
    mine = jnp.broadcast_to(turn[pl.ds(me, 1), :], (HALF, 128))
    spot = lax.broadcasted_iota(jnp.int32, (HALF, 128), 0)
    first = jnp.sum(jnp.where(lane((HALF, 128)) == spot, mine, 0.0), axis=1, keepdims=True)
    second = jnp.sum(jnp.where(lane((HALF, 128)) == spot + HALF, mine, 0.0), axis=1, keepdims=True)
    own_bits = jnp.where(low_half, first, second)
    own_scale[...] = jnp.where(own_bits > 0.5, DOWN, UP)

    for load in loads:
        load.wait()

    def send_out(chunk):
        def one(k, carry):
            peer = lax.rem(me + k, PEERS)
            pltpu.make_async_remote_copy(
                src_ref=outgoing.at[pl.ds(pl.multiple_of(peer * PITCH_OUT + chunk * PER_CHUNK, 8), PER_CHUNK), :],
                dst_ref=arrived.at[me, pl.ds(pl.multiple_of(chunk * PER_CHUNK, 8), PER_CHUNK), :],
                send_sem=send_sem,
                recv_sem=recv_sems.at[me],
                device_id={"cols": peer},
                device_id_type=MESH,
            ).start()
            return carry

        lax.fori_loop(1, PEERS, one, 0)

    def left_chunk(chunk):
        base = chunk * PER_CHUNK
        tiles = []
        for k in range(PER_CHUNK):
            pair = (
                held[pl.ds(base + k, HALF, stride=PITCH_IN), :],
                held[pl.ds(base + k + HALF, HALF, stride=PITCH_IN), :],
            )
            tiles.append(rows_of_pair(pair))
        for moment in range(SLICES):
            scale = gain[moment * L : (moment + 1) * L, :]
            pairs = []
            for k in range(0, PER_CHUNK, 2):
                pairs.append(jnp.concatenate([tiles[k] * scale, tiles[k + 1] * scale], axis=0))
            pairs = [mix_lanes(pair, lanes_ref[...]) for pair in pairs]
            weights = last_ref if moment == SLICES - 1 else left_ref
            mixed = [mix_rows(weights[...], beside([pair[:L], pair[L:]])) for pair in pairs]
            tiles = [half for pair in mixed for half in (pair[:, :128], pair[:, 128:])]
        for k in range(PER_CHUNK):
            row = own_scale[pl.ds(base + k, 1), :]
            outgoing[pl.ds(base + k, L, stride=PITCH_OUT), :] = tiles[k] * row

    def left_step(chunk, carry):
        left_chunk(chunk)

        @pl.when(chunk == 0)
        def _():
            pl.semaphore_wait(barrier, PEERS - 1)

        send_out(chunk)
        return carry

    lax.fori_loop(0, CHUNKS, left_step, 0)

    arrived[me] = outgoing[pl.ds(pl.multiple_of(me * PITCH_OUT, 8), HALF), :]

    def spread(k, carry):
        at = lane((128, 128))
        pick_y = jnp.where(at < 64, k, k + HALF)
        pick_x = jnp.where(at < 64, 2 * k, 2 * k + 1)
        from_row = lax.broadcasted_iota(jnp.int32, (128, 128), 0)
        hot_y = (from_row == pick_y).astype(jnp.bfloat16)
        hot_x = (from_row == pick_x).astype(jnp.bfloat16)
        wide_y = jnp.dot(turn[L : 2 * L, :].astype(jnp.bfloat16), hot_y, preferred_element_type=jnp.float32)
        wide_x = jnp.dot(turn[3 * L : 4 * L, :].astype(jnp.bfloat16), hot_x, preferred_element_type=jnp.float32)
        scale_x[k] = jnp.where(wide_y > 0.5, DOWN, UP)
        scale_y[k] = jnp.where(wide_x > 0.5, DOWN, UP)
        return carry

    square = jnp.concatenate([turn[2 * L : 3 * L, :], jnp.zeros((L, 128), jnp.float32)], axis=0)
    turn[3 * L : 4 * L, :] = square.T[:L, :]
    lax.fori_loop(0, HALF, spread, 0)

    weights = right_ref
    group = 4

    def wait_block(sems, buffer, peer):
        @pl.when(peer != me)
        def _():
            pltpu.make_async_remote_copy(
                src_ref=buffer.at[peer],
                dst_ref=buffer.at[peer],
                send_sem=send_sem,
                recv_sem=sems.at[peer],
                device_id={"cols": peer},
                device_id_type=MESH,
            ).wait_recv()

    def by_lines(step, carry):
        spots = [lax.rem(me // 2 + 2 * HALF - step * group - k, HALF) for k in range(group)]
        for spot in spots:
            for q in range(2):
                wait_block(recv_sems, arrived, 2 * spot + q)
        tiles = [rows_of_pair((arrived[2 * spot], arrived[2 * spot + 1])) for spot in spots]
        mixed = [mix_rows(weights[...], beside(tiles[k : k + 2])) for k in range(0, group, 2)]
        tiles = [half for pair in mixed for half in (pair[:, :128], pair[:, 128:])]
        for spot, tile in zip(spots, tiles):
            even, odd = pair_of_rows(tile)
            lines[pl.ds(2 * spot, HALF, stride=PITCH_X), :] = even
            lines[pl.ds(2 * spot + 1, HALF, stride=PITCH_X), :] = odd
        return carry

    lax.fori_loop(0, HALF // group, by_lines, 0)

    def across(step, carry):
        spots = [step * group + k for k in range(group)]
        tiles = [lines[pl.ds(pl.multiple_of(spot * PITCH_X, 8), L), :] for spot in spots]
        mixed = [mix_rows(weights[...], beside(tiles[k : k + 2])) for k in range(0, group, 2)]
        scaled = [
            pair * beside([scale_x[spots[2 * k]], scale_x[spots[2 * k + 1]]]) for k, pair in enumerate(mixed)
        ]
        mixed = [mix_rows(weights[...], pair) for pair in scaled]
        tiles = [half for pair in mixed for half in (pair[:, :128], pair[:, 128:])]
        for spot, tile in zip(spots, tiles):
            lines[pl.ds(pl.multiple_of(spot * PITCH_X, 8), L), :] = tile
        return carry

    lax.fori_loop(0, HALF // group, across, 0)

    def along(step, carry):
        spots = [step * group + k for k in range(group)]
        tiles = [
            rows_of_pair(
                (
                    lines[pl.ds(2 * spot, HALF, stride=PITCH_X), :],
                    lines[pl.ds(2 * spot + 1, HALF, stride=PITCH_X), :],
                )
            )
            for spot in spots
        ]
        mixed = [mix_rows(weights[...], beside(tiles[k : k + 2])) for k in range(0, group, 2)]
        scaled = [
            pair * beside([scale_y[spots[2 * k]], scale_y[spots[2 * k + 1]]]) for k, pair in enumerate(mixed)
        ]
        mixed = [mix_rows(weights[...], pair) for pair in scaled]
        tiles = [half for pair in mixed for half in (pair[:, :128], pair[:, 128:])]
        for spot, tile in zip(spots, tiles):
            even, odd = pair_of_rows(tile)
            lines[pl.ds(2 * spot, HALF, stride=PITCH_X), :] = even
            lines[pl.ds(2 * spot + 1, HALF, stride=PITCH_X), :] = odd
        return carry

    lax.fori_loop(0, HALF // group, along, 0)

    def send_back(chunk):
        def one(k, carry):
            peer = lax.rem(me + k, PEERS)
            pltpu.make_async_remote_copy(
                src_ref=returning.at[pl.ds(pl.multiple_of(peer * PITCH_OUT + chunk * PER_CHUNK, 8), PER_CHUNK), :],
                dst_ref=landed.at[me, pl.ds(pl.multiple_of(chunk * PER_CHUNK, 8), PER_CHUNK), :],
                send_sem=back_send_sem,
                recv_sem=back_recv_sems.at[me],
                device_id={"cols": peer},
                device_id_type=MESH,
            ).start()
            return carry

        lax.fori_loop(1, PEERS, one, 0)

    def finish(chunk, carry):
        base = chunk * PER_CHUNK
        tiles = [lines[pl.ds(pl.multiple_of((base + k) * PITCH_X, 8), L), :] for k in range(PER_CHUNK)]
        mixed = [mix_rows(weights[...], beside(tiles[k : k + 2])) for k in range(0, PER_CHUNK, 2)]
        tiles = [half for pair in mixed for half in (pair[:, :128], pair[:, 128:])]
        for k, tile in enumerate(tiles):
            returning[pl.ds(base + k, L, stride=PITCH_OUT), :] = tile
        send_back(chunk)
        return carry

    lax.fori_loop(0, CHUNKS, finish, 0)

    landed[me] = returning[pl.ds(pl.multiple_of(me * PITCH_OUT, 8), HALF), :]

    def merge(step, carry):
        spot = lax.rem(me // 2 + 2 * HALF - step, HALF)
        for q in range(2):
            wait_block(back_recv_sems, landed, 2 * spot + q)
        upper, lower = swap_halves(landed[2 * spot], landed[2 * spot + 1])
        columns = pl.ds(pl.multiple_of(spot * 128, 128), 128)
        out_ref[0:HALF, columns] = upper
        out_ref[HALF:L, columns] = lower
        return carry

    lax.fori_loop(0, HALF, merge, 0)

    for buffer, sem in ((arrived, send_sem), (landed, back_send_sem)):
        everything = buffer.at[pl.ds(0, PEERS - 1)]
        pltpu.make_async_remote_copy(
            src_ref=everything,
            dst_ref=everything,
            send_sem=sem,
            recv_sem=recv_sems.at[0],
            device_id={"cols": lax.rem(me + 1, PEERS)},
            device_id_type=MESH,
        ).wait_send()


def shards(green_by_column, field):
    green = green_by_column.reshape(L, SITES)
    bits = field.reshape(SLICES, SITES)
    order = np.concatenate([np.arange(0, L, 2), np.arange(1, L, 2)])
    forward = circulant(hop_rate)
    inverse = circulant(-hop_rate)
    left = jnp.asarray(as_left(forward[np.ix_(order, order)]))
    last = jnp.asarray(as_left(forward[:, order]))
    lanes = jnp.asarray(as_right(forward))
    right = jnp.asarray(as_left(inverse))
    vmem = pl.BlockSpec(memory_space=pltpu.VMEM)
    wrapped = pl.pallas_call(
        kernel,
        out_shape=jax.ShapeDtypeStruct((L, SITES), jnp.float32),
        in_specs=[pl.BlockSpec(memory_space=pl.ANY)] + [vmem] * 5,
        out_specs=vmem,
        scratch_shapes=[
            pltpu.VMEM((HALF * PITCH_IN, 128), jnp.float32),
            pltpu.VMEM((SLICES * HALF, 128), jnp.float32),
            pltpu.VMEM((SLICES * L, 128), jnp.float32),
            pltpu.VMEM((4 * L, 128), jnp.float32),
            pltpu.VMEM((HALF, 128), jnp.float32),
            pltpu.VMEM((HALF, L, 128), jnp.float32),
            pltpu.VMEM((HALF, L, 128), jnp.float32),
            pltpu.VMEM((PEERS * PITCH_OUT, 128), jnp.float32),
            pltpu.VMEM((PEERS, HALF, 128), jnp.float32),
            pltpu.VMEM((HALF * PITCH_X, 128), jnp.float32),
            pltpu.VMEM((PEERS * PITCH_OUT, 128), jnp.float32),
            pltpu.VMEM((PEERS, HALF, 128), jnp.float32),
            pltpu.SemaphoreType.DMA((HALF,)),
            pltpu.SemaphoreType.DMA,
            pltpu.SemaphoreType.DMA((PEERS,)),
            pltpu.SemaphoreType.DMA,
            pltpu.SemaphoreType.DMA((PEERS,)),
        ],
        compiler_params=pltpu.CompilerParams(collective_id=0, has_side_effects=True),
    )(green, bits, left, last, lanes, right)
    return wrapped.reshape(1, L, SITES)


def solution(mesh):
    return jax.shard_map(
        shards,
        mesh=mesh,
        in_specs=(P("walk", "cols", None), P("walk", None, None)),
        out_specs=P("walk", "cols", None),
        check_vma=False,
    )
```

profile of v0, /device:TPU:2, one launch (start us, length us, event | category | flops | bytes accessed | tf_op | source)
XLA Modules:
  0.0 77.6 jit_solution(24488478231742520)
XLA Ops:
  0.0 1.5 %copy.9 = s32[1,3,4096]{2,1,0:T(4,128)} copy(s32[1,3,4096]{2,0,1:T(1,128)} %param.7) | data formatting | bytes 98304
  1.5 73.9 %shard_map.64 = f32[64,4096]{1,0:T(8,128)} custom-call(f32[64,4096]{1,0:T(8,128)} %bitcast.6, s32[3,4096]{1,0:T(4,128)} %bitcast.7, bf16[64,192]{1,0:T(8,128)(2,1)} %constant.8.clone.left_ref, bf16[64,192]{1,0:T(8,128)(2,1)} %constant.9.clone.last_ref, bf16[256,256]{1,0:T(8,128)(2,1)} %constant.10.clone.lanes_ref, bf16[64,192]{1,0:T(8,128)(2,1)} %constant.11.clone.right_ref), custom_call_target="tpu_custom_call" | custom-call | tf_op jit(solution)/shard_map/pallas_call | solution.py:353
  75.4 2.3 %copy.11 = f32[1,64,4096]{2,1,0:T(8,128)} copy(f32[1,64,4096]{2,1,0:T(8,128)} %bitcast.5) | data formatting | bytes 2097152
where the time goes:
time: 78.2 us; the launch traced here: 77.6 us
  Pallas kernels  73.9 us (95%)
  local copies, waits for them, and re-layouts  3.73 us (5%)
    pallas_call x1, Pallas kernels, shards(): pl.pallas_call(kernel, out_shape=jax.ShapeDtypeStruct((L, SITES), jnp.flo...  73.9 us
    unnamed x2, local copies, waits for them, and re-layouts  3.73 us

commit v1 on v0

v1 whole, which is shorter than its diff:
```python
import jax
import jax.numpy as jnp
import numpy as np
from jax import lax
from jax.experimental import pallas as pl
from jax.experimental.pallas import tpu as pltpu
from jax.sharding import PartitionSpec as P

L = 64
SITES = L * L
SLICES = 3
PEERS = 64
TILES = SITES // 128
BLOCKS = 4
ROWS = L // BLOCKS
HALVES = 2
STEPS = 4
PER_STEP = ROWS // STEPS
PITCH_IN = 72
PITCH_OUT = 24
PITCH_X = 72

hop_rate = 0.6
coupling = 0.65373
UP = float(np.exp(coupling))
DOWN = float(np.exp(-coupling))

MESH = pl.DeviceIdType.MESH


def circulant(rate):
    k = np.arange(L)
    spectrum = np.exp(rate * np.cos(2.0 * np.pi * k / L))
    differ = k[:, None] - k[None, :]
    waves = np.cos(2.0 * np.pi * (differ[:, :, None] * k) / L)
    return (waves * spectrum).sum(-1) / L


def high_low(matrix):
    matrix = matrix.astype(np.float32)
    high = matrix.astype(jnp.bfloat16)
    low = (matrix - high.astype(np.float32)).astype(jnp.bfloat16)
    return high, low


def as_left(matrix):
    high, low = high_low(matrix)
    return np.concatenate([high, low, high], axis=1)


def as_right(matrix, columns):
    both = np.kron(np.eye(2), matrix)[:, columns]
    high, low = high_low(both)
    upper = np.concatenate([high, low], axis=1)
    lower = np.concatenate([high, np.zeros_like(low)], axis=1)
    return np.concatenate([upper, lower], axis=0)


def split(values):
    high = values.astype(jnp.bfloat16)
    low = (values - high.astype(jnp.float32)).astype(jnp.bfloat16)
    return high, low


def mix_rows(weights, values):
    high, low = split(values)
    stacked = jnp.concatenate([high, high, low], axis=0)
    return jnp.dot(weights, stacked, preferred_element_type=jnp.float32)


def mix_lanes(values, weights):
    high, low = split(values)
    wide = jnp.concatenate([high, low], axis=1)
    both = jnp.dot(wide, weights, preferred_element_type=jnp.float32)
    return both[:, :128] + both[:, 128:]


def lane(shape):
    return lax.broadcasted_iota(jnp.int32, shape, len(shape) - 1)


def swap_lanes(first, second, width):
    keep = (lane(first.shape) // width) % 2 == 0
    return (
        jnp.where(keep, first, pltpu.roll(second, width, 1)),
        jnp.where(keep, pltpu.roll(first, 128 - width, 1), second),
    )


def swap_blocks(tiles):
    t0, t2 = swap_lanes(tiles[0], tiles[2], 64)
    t1, t3 = swap_lanes(tiles[1], tiles[3], 64)
    t0, t1 = swap_lanes(t0, t1, 32)
    t2, t3 = swap_lanes(t2, t3, 32)
    return [t0, t1, t2, t3]


def rows_of_tiles(tiles):
    return jnp.concatenate(swap_blocks(tiles), axis=0)


def tiles_of_rows(rows):
    return swap_blocks([rows[k * ROWS : (k + 1) * ROWS] for k in range(BLOCKS)])


def beside(tiles):
    return jnp.concatenate(tiles, axis=1)


def mix_tiles(weights, tiles):
    mixed = [mix_rows(weights, beside(tiles[k : k + 2])) for k in range(0, len(tiles), 2)]
    return [half for pair in mixed for half in (pair[:, :128], pair[:, 128:])]


def kernel(
    green_ref, field_ref, left_ref, last_ref, lanes_ref, lanes_last_ref, right_ref, out_ref,
    held, gain, turn, own_scale, scale_x, scale_y,
    outgoing, arrived, lines, returning, landed,
    load_sems, send_sem, recv_sems, back_send_sem, back_recv_sems,
):
    me = lax.axis_index("cols")
    barrier = pltpu.get_barrier_semaphore()

    loads = [
        pltpu.make_async_copy(
            green_ref.at[:, pl.ds(t * 128, 128)],
            held.at[pl.ds(t * PITCH_IN, L), :],
            load_sems.at[t],
        )
        for t in range(TILES)
    ]
    for load in loads:
        load.start()

    def greet(k, carry):
        pl.semaphore_signal(
            barrier, inc=1, device_id={"cols": lax.rem(me + k, PEERS)}, device_id_type=MESH
        )
        return carry

    lax.fori_loop(1, PEERS, greet, 0)

    low_half = lane((TILES, 128)) < 64
    for moment in range(SLICES):
        bits = field_ref[moment * TILES : (moment + 1) * TILES, :].astype(jnp.float32)
        turned = pltpu.roll(bits, 64, 1)
        even = jnp.where(low_half, bits, turned)
        odd = jnp.where(low_half, turned, bits)
        gain[moment * L : moment * L + TILES, :] = jnp.where(even > 0.5, UP, DOWN)
        gain[moment * L + TILES : (moment + 1) * L, :] = jnp.where(odd > 0.5, UP, DOWN)
        turn[pl.ds(moment * L, TILES, stride=2), :] = bits
        turn[pl.ds(moment * L + 1, TILES, stride=2), :] = turned
    mine = jnp.broadcast_to(turn[pl.ds(me, 1), :], (ROWS, 128))
    site = lane((ROWS, 128))
    spot_row = lax.broadcasted_iota(jnp.int32, (ROWS, 128), 0)
    own_bits = jnp.zeros((ROWS, 128), jnp.float32)
    for block in range(BLOCKS):
        picked = jnp.where(site == spot_row + block * ROWS, mine, 0.0)
        own_bits = jnp.where(site // 32 == block, jnp.sum(picked, axis=1, keepdims=True), own_bits)
    own_scale[...] = jnp.where(own_bits > 0.5, DOWN, UP)

    for load in loads:
        load.wait()

    def send_out(half, start, count):
        def one(k, carry):
            peer = lax.rem(me + k, PEERS)
            pltpu.make_async_remote_copy(
                src_ref=outgoing.at[pl.ds(pl.multiple_of((half * PEERS + peer) * PITCH_OUT + start, 8), count), :],
                dst_ref=arrived.at[half * PEERS + me, pl.ds(start, count), :],
                send_sem=send_sem,
                recv_sem=recv_sems.at[half * PEERS + me],
                device_id={"cols": peer},
                device_id_type=MESH,
            ).start()
            return carry

        lax.fori_loop(1, PEERS, one, 0)

    def left_step(step, carry):
        base = step * PER_STEP
        tiles = []
        for k in range(PER_STEP):
            for upper in range(2):
                row = base + k + upper * 2 * ROWS
                pair = swap_lanes(
                    held[pl.ds(row, TILES, stride=PITCH_IN), :],
                    held[pl.ds(row + ROWS, TILES, stride=PITCH_IN), :],
                    64,
                )
                tiles.append(jnp.concatenate(pair, axis=0))
        for moment in range(SLICES):
            ends = moment == SLICES - 1
            scale = gain[moment * L : (moment + 1) * L, :]
            tiles = mix_tiles((last_ref if ends else left_ref)[...], [tile * scale for tile in tiles])
            weights = (lanes_last_ref if ends else lanes_ref)[...]
            pairs = [
                mix_lanes(jnp.concatenate(tiles[k : k + 2], axis=0), weights) for k in range(0, len(tiles), 2)
            ]
            tiles = [part for pair in pairs for part in (pair[:L], pair[L:])]
        for k in range(PER_STEP):
            row = own_scale[pl.ds(base + k, 1), :]
            for half, tile in enumerate(swap_lanes(tiles[2 * k], tiles[2 * k + 1], 64)):
                outgoing[pl.ds(half * PEERS * PITCH_OUT + base + k, L, stride=PITCH_OUT), :] = tile * row
        return carry

    lax.fori_loop(0, STEPS // 2, left_step, 0)
    pl.semaphore_wait(barrier, PEERS - 1)
    send_out(0, 0, ROWS // 2)
    lax.fori_loop(STEPS // 2, STEPS, left_step, 0)
    send_out(0, ROWS // 2, ROWS // 2)
    send_out(1, 0, ROWS)

    for half in range(HALVES):
        arrived[half * PEERS + me] = outgoing[pl.ds(pl.multiple_of((half * PEERS + me) * PITCH_OUT, 8), ROWS), :]

    square = jnp.concatenate([turn[2 * L : 3 * L, :], jnp.zeros((L, 128), jnp.float32)], axis=0)
    turn[3 * L : 4 * L, :] = square.T[:L, :]

    def spread(k, carry):
        block = lane((128, 128)) // 32
        from_row = lax.broadcasted_iota(jnp.int32, (128, 128), 0)
        hot_y = (from_row == block * ROWS + k).astype(jnp.bfloat16)
        hot_x = (from_row == block + k * BLOCKS).astype(jnp.bfloat16)
        wide_y = jnp.dot(turn[L : 2 * L, :].astype(jnp.bfloat16), hot_y, preferred_element_type=jnp.float32)
        wide_x = jnp.dot(turn[3 * L : 4 * L, :].astype(jnp.bfloat16), hot_x, preferred_element_type=jnp.float32)
        scale_x[k] = jnp.where(wide_y > 0.5, DOWN, UP)
        scale_y[k] = jnp.where(wide_x > 0.5, DOWN, UP)
        return carry

    lax.fori_loop(0, ROWS, spread, 0)

    def wait_block(sems, buffer, half, peer):
        @pl.when(peer != me)
        def _():
            at = half * PEERS + peer
            pltpu.make_async_remote_copy(
                src_ref=buffer.at[at],
                dst_ref=buffer.at[at],
                send_sem=send_sem,
                recv_sem=sems.at[at],
                device_id={"cols": peer},
                device_id_type=MESH,
            ).wait_recv()

    group = 8

    def right_half(half, carry):
        weights = right_ref[...]

        def store_lines(spots, tiles):
            for spot, rows in zip(spots, tiles):
                for k, tile in enumerate(tiles_of_rows(rows)):
                    lines[pl.ds(spot * BLOCKS + k, ROWS, stride=PITCH_X), :] = tile

        def by_lines(step, carry):
            spots = [lax.rem(me // BLOCKS + 2 * ROWS - step * group - k, ROWS) for k in range(group)]
            for spot in spots:
                for k in range(BLOCKS):
                    wait_block(recv_sems, arrived, half, spot * BLOCKS + k)
            tiles = [
                rows_of_tiles([arrived[half * PEERS + spot * BLOCKS + k] for k in range(BLOCKS)]) for spot in spots
            ]
            store_lines(spots, mix_tiles(weights, tiles))
            return carry

        lax.fori_loop(0, ROWS // group, by_lines, 0)

        def across(step, carry):
            spots = [step * group + k for k in range(group)]
            tiles = [lines[pl.ds(pl.multiple_of(spot * PITCH_X, 8), L), :] for spot in spots]
            tiles = mix_tiles(weights, tiles)
            tiles = mix_tiles(weights, [tile * scale_x[spot] for spot, tile in zip(spots, tiles)])
            for spot, tile in zip(spots, tiles):
                lines[pl.ds(pl.multiple_of(spot * PITCH_X, 8), L), :] = tile
            return carry

        lax.fori_loop(0, ROWS // group, across, 0)

        def along(step, carry):
            spots = [step * group + k for k in range(group)]
            tiles = [
                rows_of_tiles([lines[pl.ds(spot * BLOCKS + k, ROWS, stride=PITCH_X), :] for k in range(BLOCKS)])
                for spot in spots
            ]
            tiles = mix_tiles(weights, tiles)
            tiles = mix_tiles(weights, [tile * scale_y[spot] for spot, tile in zip(spots, tiles)])
            store_lines(spots, tiles)
            return carry

        lax.fori_loop(0, ROWS // group, along, 0)

        def finish(step, carry):
            spots = [step * group + k for k in range(group)]
            tiles = [lines[pl.ds(pl.multiple_of(spot * PITCH_X, 8), L), :] for spot in spots]
            for spot, tile in zip(spots, mix_tiles(weights, tiles)):
                returning[pl.ds(half * PEERS * PITCH_OUT + spot, L, stride=PITCH_OUT), :] = tile
            return carry

        lax.fori_loop(0, ROWS // group, finish, 0)

        def send_back(k, carry):
            peer = lax.rem(me + k, PEERS)
            pltpu.make_async_remote_copy(
                src_ref=returning.at[pl.ds(pl.multiple_of((half * PEERS + peer) * PITCH_OUT, 8), ROWS), :],
                dst_ref=landed.at[half * PEERS + me],
                send_sem=back_send_sem,
                recv_sem=back_recv_sems.at[half * PEERS + me],
                device_id={"cols": peer},
                device_id_type=MESH,
            ).start()
            return carry

        lax.fori_loop(1, PEERS, send_back, 0)
        landed[half * PEERS + me] = returning[pl.ds(pl.multiple_of((half * PEERS + me) * PITCH_OUT, 8), ROWS), :]
        return carry

    lax.fori_loop(0, HALVES, right_half, 0)

    together = 4

    def merge(step, carry):
        spots = [lax.rem(me // 2 + 2 * TILES - step * together - k, TILES) for k in range(together)]
        for spot in spots:
            for q in range(2):
                for half in range(HALVES):
                    wait_block(back_recv_sems, landed, half, 2 * spot + q)
        for spot in spots:
            tiles = [landed[half * PEERS + 2 * spot + q] for q in range(2) for half in range(HALVES)]
            columns = pl.ds(pl.multiple_of(spot * 128, 128), 128)
            for k, tile in enumerate(swap_blocks(tiles)):
                out_ref[k * ROWS : (k + 1) * ROWS, columns] = tile
        return carry

    lax.fori_loop(0, TILES // together, merge, 0)

    for buffer, sem in ((arrived, send_sem), (landed, back_send_sem)):
        everything = buffer.at[pl.ds(0, HALVES * (PEERS - 1))]
        pltpu.make_async_remote_copy(
            src_ref=everything,
            dst_ref=everything,
            send_sem=sem,
            recv_sem=recv_sems.at[0],
            device_id={"cols": lax.rem(me + 1, PEERS)},
            device_id_type=MESH,
        ).wait_send()


def shards(green_by_column, field):
    green = green_by_column.reshape(L, SITES)
    bits = field.reshape(SLICES * TILES, 128)
    order = np.concatenate([np.arange(0, L, 2), np.arange(1, L, 2)])
    columns = np.arange(128).reshape(2, HALVES, 32).transpose(1, 0, 2).reshape(128)
    forward = circulant(hop_rate)
    inverse = circulant(-hop_rate)
    left = jnp.asarray(as_left(forward[np.ix_(order, order)]))
    last = jnp.asarray(as_left(forward[:, order]))
    lanes = jnp.asarray(as_right(forward, np.arange(128)))
    lanes_last = jnp.asarray(as_right(forward, columns))
    right = jnp.asarray(as_left(inverse))
    vmem = pl.BlockSpec(memory_space=pltpu.VMEM)
    wrapped = pl.pallas_call(
        kernel,
        out_shape=jax.ShapeDtypeStruct((L, SITES), jnp.float32),
        in_specs=[pl.BlockSpec(memory_space=pl.ANY)] + [vmem] * 6,
        out_specs=vmem,
        scratch_shapes=[
            pltpu.VMEM((TILES * PITCH_IN, 128), jnp.float32),
            pltpu.VMEM((SLICES * L, 128), jnp.float32),
            pltpu.VMEM((4 * L, 128), jnp.float32),
            pltpu.VMEM((ROWS, 128), jnp.float32),
            pltpu.VMEM((ROWS, L, 128), jnp.float32),
            pltpu.VMEM((ROWS, L, 128), jnp.float32),
            pltpu.VMEM((HALVES * PEERS * PITCH_OUT, 128), jnp.float32),
            pltpu.VMEM((HALVES * PEERS, ROWS, 128), jnp.float32),
            pltpu.VMEM((ROWS * PITCH_X, 128), jnp.float32),
            pltpu.VMEM((HALVES * PEERS * PITCH_OUT, 128), jnp.float32),
            pltpu.VMEM((HALVES * PEERS, ROWS, 128), jnp.float32),
            pltpu.SemaphoreType.DMA((TILES,)),
            pltpu.SemaphoreType.DMA,
            pltpu.SemaphoreType.DMA((HALVES * PEERS,)),
            pltpu.SemaphoreType.DMA,
            pltpu.SemaphoreType.DMA((HALVES * PEERS,)),
        ],
        compiler_params=pltpu.CompilerParams(collective_id=0, has_side_effects=True),
    )(green, bits, left, last, lanes, lanes_last, right)
    return wrapped.reshape(1, L, SITES)


def solution(mesh):
    return jax.shard_map(
        shards,
        mesh=mesh,
        in_specs=(P("walk", "cols", None), P("walk", None, None)),
        out_specs=P("walk", "cols", None),
        check_vma=False,
    )
```

time: 78.2 us -> 64.7 us (0.83)
  Pallas kernels: 73.9 us -> 62.3 us
  local copies, waits for them, and re-layouts: 3.73 us -> 2.27 us
    pallas_call x1, Pallas kernels: 73.9 us -> 62.3 us  [shards(): pl.pallas_call(kernel, out_shape=jax.ShapeDtypeStruct((L, SITES), jnp.flo...]
    unnamed x2 -> x1, local copies, waits for them, and re-layouts: 3.73 us -> 2.27 us
where the time goes in v1:
time: 64.7 us; the launch traced here: 64.5 us
  Pallas kernels  62.3 us (96%)
  local copies, waits for them, and re-layouts  2.27 us (4%)
    pallas_call x1, Pallas kernels, shards(): pl.pallas_call(kernel, out_shape=jax.ShapeDtypeStruct((L, SITES), jnp.flo...  62.3 us
    unnamed x1, local copies, waits for them, and re-layouts  2.27 us

profile of v1, /device:TPU:2, one launch (start us, length us, event | category | flops | bytes accessed | tf_op | source)
XLA Modules:
  0.0 64.5 jit_solution(8719660413271827955)
XLA Ops:
  0.0 62.3 %shard_map.73 = f32[64,4096]{1,0:T(8,128)} custom-call(f32[64,4096]{1,0:T(8,128)} %bitcast.4, s32[96,128]{1,0:T(8,128)} %bitcast.5, bf16[64,192]{1,0:T(8,128)(2,1)} %constant.10.clone.left_ref, bf16[64,192]{1,0:T(8,128)(2,1)} %constant.11.clone.last_ref, bf16[256,256]{1,0:T(8,128)(2,1)} %constant.12.clone.lanes_ref, ...), custom_call_target="tpu_custom_call" | custom-call | tf_op jit(solution)/shard_map/pallas_call | solution.py:362
  62.3 2.3 %copy.9 = f32[1,64,4096]{2,1,0:T(8,128)} copy(f32[1,64,4096]{2,1,0:T(8,128)} %bitcast.3) | data formatting | bytes 2097152

commit v2 on v1

--- a/solution.py
+++ b/solution.py
@@ -14,8 +14,10 @@
 BLOCKS = 4
 ROWS = L // BLOCKS
 HALVES = 2
-STEPS = 4
+STEPS = 2
 PER_STEP = ROWS // STEPS
+GROUP = 8
+MERGED = 4
 PITCH_IN = 72
 PITCH_OUT = 24
 PITCH_X = 72
@@ -113,10 +115,10 @@
 
 
 def kernel(
-    green_ref, field_ref, left_ref, last_ref, lanes_ref, lanes_last_ref, right_ref, out_ref,
-    held, gain, turn, own_scale, scale_x, scale_y,
+    green_ref, field_hbm, left_hbm, last_hbm, lanes_hbm, lanes_last_hbm, right_hbm, out_ref,
+    field_ref, left_ref, last_ref, lanes_ref, lanes_last_ref, right_ref, held, gain, turn, own_scale, scale_x, scale_y,
     outgoing, arrived, lines, returning, landed,
-    load_sems, send_sem, recv_sems, back_send_sem, back_recv_sems,
+    small_sems, load_sem, send_sem, recv_sems, back_send_sem, back_recv_sems,
 ):
     me = lax.axis_index("cols")
     barrier = pltpu.get_barrier_semaphore()
@@ -125,12 +127,28 @@
         pltpu.make_async_copy(
             green_ref.at[:, pl.ds(t * 128, 128)],
             held.at[pl.ds(t * PITCH_IN, L), :],
-            load_sems.at[t],
+            load_sem,
         )
         for t in range(TILES)
     ]
+    smalls = [
+        pltpu.make_async_copy(source, target, small_sems.at[k])
+        for k, (source, target) in enumerate(
+            [
+                (field_hbm, field_ref),
+                (left_hbm, left_ref),
+                (lanes_hbm, lanes_ref),
+                (last_hbm, last_ref),
+                (lanes_last_hbm, lanes_last_ref),
+                (right_hbm, right_ref),
+            ]
+        )
+    ]
+    smalls[0].start()
     for load in loads:
         load.start()
+    for small in smalls[1:]:
+        small.start()
 
     def greet(k, carry):
         pl.semaphore_signal(
@@ -140,6 +158,7 @@
 
     lax.fori_loop(1, PEERS, greet, 0)
 
+    smalls[0].wait()
     low_half = lane((TILES, 128)) < 64
     for moment in range(SLICES):
         bits = field_ref[moment * TILES : (moment + 1) * TILES, :].astype(jnp.float32)
@@ -159,17 +178,18 @@
         own_bits = jnp.where(site // 32 == block, jnp.sum(picked, axis=1, keepdims=True), own_bits)
     own_scale[...] = jnp.where(own_bits > 0.5, DOWN, UP)
 
-    for load in loads:
-        load.wait()
+    for small in smalls[1:]:
+        small.wait()
+    pltpu.make_async_copy(arrived, arrived, load_sem).wait()
 
     def send_out(half, start, count):
         def one(k, carry):
             peer = lax.rem(me + k, PEERS)
             pltpu.make_async_remote_copy(
                 src_ref=outgoing.at[pl.ds(pl.multiple_of((half * PEERS + peer) * PITCH_OUT + start, 8), count), :],
-                dst_ref=arrived.at[half * PEERS + me, pl.ds(start, count), :],
+                dst_ref=arrived.at[half * PEERS + me, pl.ds(pl.multiple_of(start, 8), count), :],
                 send_sem=send_sem,
-                recv_sem=recv_sems.at[half * PEERS + me],
+                recv_sem=recv_sems.at[half * 2 + lax.rem(peer // BLOCKS + ROWS - me // BLOCKS, ROWS) // GROUP],
                 device_id={"cols": peer},
                 device_id_type=MESH,
             ).start()
@@ -194,21 +214,21 @@
             scale = gain[moment * L : (moment + 1) * L, :]
             tiles = mix_tiles((last_ref if ends else left_ref)[...], [tile * scale for tile in tiles])
             weights = (lanes_last_ref if ends else lanes_ref)[...]
-            pairs = [
-                mix_lanes(jnp.concatenate(tiles[k : k + 2], axis=0), weights) for k in range(0, len(tiles), 2)
-            ]
-            tiles = [part for pair in pairs for part in (pair[:L], pair[L:])]
+            stack = mix_lanes(jnp.concatenate(tiles, axis=0), weights)
+            tiles = [stack[k * L : (k + 1) * L] for k in range(len(tiles))]
         for k in range(PER_STEP):
             row = own_scale[pl.ds(base + k, 1), :]
             for half, tile in enumerate(swap_lanes(tiles[2 * k], tiles[2 * k + 1], 64)):
                 outgoing[pl.ds(half * PEERS * PITCH_OUT + base + k, L, stride=PITCH_OUT), :] = tile * row
+
+        @pl.when(step == 0)
+        def _():
+            pl.semaphore_wait(barrier, PEERS - 1)
+
+        send_out(0, base, PER_STEP)
         return carry
 
-    lax.fori_loop(0, STEPS // 2, left_step, 0)
-    pl.semaphore_wait(barrier, PEERS - 1)
-    send_out(0, 0, ROWS // 2)
-    lax.fori_loop(STEPS // 2, STEPS, left_step, 0)
-    send_out(0, ROWS // 2, ROWS // 2)
+    lax.fori_loop(0, STEPS, left_step, 0)
     send_out(1, 0, ROWS)
 
     for half in range(HALVES):
@@ -230,20 +250,27 @@
 
     lax.fori_loop(0, ROWS, spread, 0)
 
-    def wait_block(sems, buffer, half, peer):
-        @pl.when(peer != me)
+    def wait_blocks(sem, buffer, count):
+        blocks = buffer.at[pl.ds(0, count)]
+        pltpu.make_async_remote_copy(
+            src_ref=blocks,
+            dst_ref=blocks,
+            send_sem=send_sem,
+            recv_sem=sem,
+            device_id={"cols": lax.rem(me + 1, PEERS)},
+            device_id_type=MESH,
+        ).wait_recv()
+
+    def wait_group(sem, buffer, step, count, own):
+        @pl.when(step == 0)
         def _():
-            at = half * PEERS + peer
-            pltpu.make_async_remote_copy(
-                src_ref=buffer.at[at],
-                dst_ref=buffer.at[at],
-                send_sem=send_sem,
-                recv_sem=sems.at[at],
-                device_id={"cols": peer},
-                device_id_type=MESH,
-            ).wait_recv()
-
-    group = 8
+            wait_blocks(sem, buffer, count - own)
+
+        @pl.when(step != 0)
+        def _():
+            wait_blocks(sem, buffer, count)
+
+    group = GROUP
 
     def right_half(half, carry):
         weights = right_ref[...]
@@ -255,9 +282,7 @@
 
         def by_lines(step, carry):
             spots = [lax.rem(me // BLOCKS + 2 * ROWS - step * group - k, ROWS) for k in range(group)]
-            for spot in spots:
-                for k in range(BLOCKS):
-                    wait_block(recv_sems, arrived, half, spot * BLOCKS + k)
+            wait_group(recv_sems.at[half * 2 + step], arrived, step, group * BLOCKS, 1)
             tiles = [
                 rows_of_tiles([arrived[half * PEERS + spot * BLOCKS + k] for k in range(BLOCKS)]) for spot in spots
             ]
@@ -305,7 +330,7 @@
                 src_ref=returning.at[pl.ds(pl.multiple_of((half * PEERS + peer) * PITCH_OUT, 8), ROWS), :],
                 dst_ref=landed.at[half * PEERS + me],
                 send_sem=back_send_sem,
-                recv_sem=back_recv_sems.at[half * PEERS + me],
+                recv_sem=back_recv_sems.at[lax.rem(peer // 2 + TILES - me // 2, TILES) // MERGED],
                 device_id={"cols": peer},
                 device_id_type=MESH,
             ).start()
@@ -317,14 +342,9 @@
 
     lax.fori_loop(0, HALVES, right_half, 0)
 
-    together = 4
-
     def merge(step, carry):
-        spots = [lax.rem(me // 2 + 2 * TILES - step * together - k, TILES) for k in range(together)]
-        for spot in spots:
-            for q in range(2):
-                for half in range(HALVES):
-                    wait_block(back_recv_sems, landed, half, 2 * spot + q)
+        spots = [lax.rem(me // 2 + 2 * TILES - step * MERGED - k, TILES) for k in range(MERGED)]
+        wait_group(back_recv_sems.at[step], landed, step, MERGED * 2 * HALVES, HALVES)
         for spot in spots:
             tiles = [landed[half * PEERS + 2 * spot + q] for q in range(2) for half in range(HALVES)]
             columns = pl.ds(pl.multiple_of(spot * 128, 128), 128)
@@ -332,7 +352,7 @@
                 out_ref[k * ROWS : (k + 1) * ROWS, columns] = tile
         return carry
 
-    lax.fori_loop(0, TILES // together, merge, 0)
+    lax.fori_loop(0, TILES // MERGED, merge, 0)
 
     for buffer, sem in ((arrived, send_sem), (landed, back_send_sem)):
         everything = buffer.at[pl.ds(0, HALVES * (PEERS - 1))]
@@ -361,10 +381,16 @@
     vmem = pl.BlockSpec(memory_space=pltpu.VMEM)
     wrapped = pl.pallas_call(
         kernel,
-        out_shape=jax.ShapeDtypeStruct((L, SITES), jnp.float32),
-        in_specs=[pl.BlockSpec(memory_space=pl.ANY)] + [vmem] * 6,
+        out_shape=pltpu.VMEM((L, SITES), jnp.float32),
+        in_specs=[pl.BlockSpec(memory_space=pl.ANY)] * 7,
         out_specs=vmem,
         scratch_shapes=[
+            pltpu.VMEM((SLICES * TILES, 128), jnp.int32),
+            pltpu.VMEM(left.shape, jnp.bfloat16),
+            pltpu.VMEM(last.shape, jnp.bfloat16),
+            pltpu.VMEM(lanes.shape, jnp.bfloat16),
+            pltpu.VMEM(lanes_last.shape, jnp.bfloat16),
+            pltpu.VMEM(right.shape, jnp.bfloat16),
             pltpu.VMEM((TILES * PITCH_IN, 128), jnp.float32),
             pltpu.VMEM((SLICES * L, 128), jnp.float32),
             pltpu.VMEM((4 * L, 128), jnp.float32),
@@ -376,11 +402,12 @@
             pltpu.VMEM((ROWS * PITCH_X, 128), jnp.float32),
             pltpu.VMEM((HALVES * PEERS * PITCH_OUT, 128), jnp.float32),
             pltpu.VMEM((HALVES * PEERS, ROWS, 128), jnp.float32),
-            pltpu.SemaphoreType.DMA((TILES,)),
+            pltpu.SemaphoreType.DMA((6,)),
             pltpu.SemaphoreType.DMA,
-            pltpu.SemaphoreType.DMA((HALVES * PEERS,)),
             pltpu.SemaphoreType.DMA,
-            pltpu.SemaphoreType.DMA((HALVES * PEERS,)),
+            pltpu.SemaphoreType.DMA((HALVES * ROWS // GROUP,)),
+            pltpu.SemaphoreType.DMA,
+            pltpu.SemaphoreType.DMA((TILES // MERGED,)),
         ],
         compiler_params=pltpu.CompilerParams(collective_id=0, has_side_effects=True),
     )(green, bits, left, last, lanes, lanes_last, right)

time: 64.7 us -> 59.5 us (0.920)
  Pallas kernels: 62.3 us -> 58.4 us
  local copies, waits for them, and re-layouts: 2.27 us -> 0.97 us
    pallas_call x1, Pallas kernels: 62.3 us -> 58.4 us  [shards(): pl.pallas_call(kernel, out_shape=pltpu.VMEM((L, SITES), jnp.float32), in_...]
    unnamed x1, local copies, waits for them, and re-layouts: 2.27 us -> 0.97 us
where the time goes in v2:
time: 59.5 us; the launch traced here: 59.4 us
  Pallas kernels  58.4 us (98%)
  local copies, waits for them, and re-layouts  0.97 us (2%)
    pallas_call x1, Pallas kernels, shards(): pl.pallas_call(kernel, out_shape=pltpu.VMEM((L, SITES), jnp.float32), in_...  58.4 us

profile of v2, /device:TPU:2, one launch (start us, length us, event | category | flops | bytes accessed | tf_op | source)
XLA Modules:
  0.0 59.4 jit_solution(3378342438184213929)
XLA Ops:
  0.0 58.4 %shard_map.73 = f32[64,4096]{1,0:T(8,128)S(1)} custom-call(f32[64,4096]{1,0:T(8,128)} %bitcast.4, s32[96,128]{1,0:T(8,128)} %bitcast.5, bf16[64,192]{1,0:T(8,128)(2,1)} %constant.10.clone.left_hbm, bf16[64,192]{1,0:T(8,128)(2,1)} %constant.11.clone.last_hbm, bf16[256,256]{1,0:T(8,128)(2,1)} %constant.12.clone.lanes_hbm, ...), custom_call_target="tpu_custom_call" | custom-call | tf_op jit(solution)/shard_map/pallas_call | solution.py:382
  58.4 1.0 %copy.9 = f32[1,64,4096]{2,1,0:T(8,128)} copy(f32[1,64,4096]{2,1,0:T(8,128)S(1)} %bitcast.3) | data formatting | bytes 2097152

commit v3 on v2

--- a/solution.py
+++ b/solution.py
@@ -122,6 +122,14 @@
 ):
     me = lax.axis_index("cols")
     barrier = pltpu.get_barrier_semaphore()
+
+    def greet(k, carry):
+        pl.semaphore_signal(
+            barrier, inc=1, device_id={"cols": lax.rem(me + k, PEERS)}, device_id_type=MESH
+        )
+        return carry
+
+    lax.fori_loop(1, PEERS, greet, 0)
 
     loads = [
         pltpu.make_async_copy(
@@ -149,14 +157,6 @@
         load.start()
     for small in smalls[1:]:
         small.start()
-
-    def greet(k, carry):
-        pl.semaphore_signal(
-            barrier, inc=1, device_id={"cols": lax.rem(me + k, PEERS)}, device_id_type=MESH
-        )
-        return carry
-
-    lax.fori_loop(1, PEERS, greet, 0)
 
     smalls[0].wait()
     low_half = lane((TILES, 128)) < 64

time: 59.5 us -> 59 us (level)
  no operation moved by 1% of the time
where the time goes in v3:
time: 59 us; the launch traced here: 58.9 us
  Pallas kernels  58 us (98%)
  local copies, waits for them, and re-layouts  0.97 us (2%)
    pallas_call x1, Pallas kernels, shards(): pl.pallas_call(kernel, out_shape=pltpu.VMEM((L, SITES), jnp.float32), in_...  58 us

profile of v3, /device:TPU:2, one launch (start us, length us, event | category | flops | bytes accessed | tf_op | source)
XLA Modules:
  0.0 58.9 jit_solution(5918949937525309648)
XLA Ops:
  0.0 58.0 %shard_map.73 = f32[64,4096]{1,0:T(8,128)S(1)} custom-call(f32[64,4096]{1,0:T(8,128)} %bitcast.4, s32[96,128]{1,0:T(8,128)} %bitcast.5, bf16[64,192]{1,0:T(8,128)(2,1)} %constant.10.clone.left_hbm, bf16[64,192]{1,0:T(8,128)(2,1)} %constant.11.clone.last_hbm, bf16[256,256]{1,0:T(8,128)(2,1)} %constant.12.clone.lanes_hbm, ...), custom_call_target="tpu_custom_call" | custom-call | tf_op jit(solution)/shard_map/pallas_call | solution.py:382
  58.0 1.0 %copy.9 = f32[1,64,4096]{2,1,0:T(8,128)} copy(f32[1,64,4096]{2,1,0:T(8,128)S(1)} %bitcast.3) | data formatting | bytes 2097152

commit v4 on v3

--- a/solution.py
+++ b/solution.py
@@ -391,16 +391,16 @@
             pltpu.VMEM(lanes.shape, jnp.bfloat16),
             pltpu.VMEM(lanes_last.shape, jnp.bfloat16),
             pltpu.VMEM(right.shape, jnp.bfloat16),
-            pltpu.VMEM((TILES * PITCH_IN, 128), jnp.float32),
+            pltpu.VMEM(((TILES + 1) * PITCH_IN, 128), jnp.float32),
             pltpu.VMEM((SLICES * L, 128), jnp.float32),
             pltpu.VMEM((4 * L, 128), jnp.float32),
             pltpu.VMEM((ROWS, 128), jnp.float32),
             pltpu.VMEM((ROWS, L, 128), jnp.float32),
             pltpu.VMEM((ROWS, L, 128), jnp.float32),
-            pltpu.VMEM((HALVES * PEERS * PITCH_OUT, 128), jnp.float32),
+            pltpu.VMEM(((HALVES * PEERS + 1) * PITCH_OUT, 128), jnp.float32),
             pltpu.VMEM((HALVES * PEERS, ROWS, 128), jnp.float32),
-            pltpu.VMEM((ROWS * PITCH_X, 128), jnp.float32),
-            pltpu.VMEM((HALVES * PEERS * PITCH_OUT, 128), jnp.float32),
+            pltpu.VMEM(((ROWS + 1) * PITCH_X, 128), jnp.float32),
+            pltpu.VMEM(((HALVES * PEERS + 1) * PITCH_OUT, 128), jnp.float32),
             pltpu.VMEM((HALVES * PEERS, ROWS, 128), jnp.float32),
             pltpu.SemaphoreType.DMA((6,)),
             pltpu.SemaphoreType.DMA,

time: 59 us -> 59 us (level)
  no operation moved by 1% of the time
where the time goes in v4:
time: 59 us; the launch traced here: 58.9 us
  Pallas kernels  58 us (98%)
  local copies, waits for them, and re-layouts  0.97 us (2%)
    pallas_call x1, Pallas kernels, shards(): pl.pallas_call(kernel, out_shape=pltpu.VMEM((L, SITES), jnp.float32), in_...  58 us

profile of v4, /device:TPU:2, one launch (start us, length us, event | category | flops | bytes accessed | tf_op | source)
XLA Modules:
  0.0 58.9 jit_solution(14264885534793417394)
XLA Ops:
  0.0 58.0 %shard_map.73 = f32[64,4096]{1,0:T(8,128)S(1)} custom-call(f32[64,4096]{1,0:T(8,128)} %bitcast.4, s32[96,128]{1,0:T(8,128)} %bitcast.5, bf16[64,192]{1,0:T(8,128)(2,1)} %constant.10.clone.left_hbm, bf16[64,192]{1,0:T(8,128)(2,1)} %constant.11.clone.last_hbm, bf16[256,256]{1,0:T(8,128)(2,1)} %constant.12.clone.lanes_hbm, ...), custom_call_target="tpu_custom_call" | custom-call | tf_op jit(solution)/shard_map/pallas_call | solution.py:382
  58.0 1.0 %copy.9 = f32[1,64,4096]{2,1,0:T(8,128)} copy(f32[1,64,4096]{2,1,0:T(8,128)S(1)} %bitcast.3) | data formatting | bytes 2097152

commit v5 on v3

--- a/solution.py
+++ b/solution.py
@@ -17,7 +17,7 @@
 STEPS = 2
 PER_STEP = ROWS // STEPS
 GROUP = 8
-MERGED = 4
+MERGED = 8
 PITCH_IN = 72
 PITCH_OUT = 24
 PITCH_X = 72
@@ -115,13 +115,15 @@
 
 
 def kernel(
-    green_ref, field_hbm, left_hbm, last_hbm, lanes_hbm, lanes_last_hbm, right_hbm, out_ref,
-    field_ref, left_ref, last_ref, lanes_ref, lanes_last_ref, right_ref, held, gain, turn, own_scale, scale_x, scale_y,
+    green_ref, field_hbm, narrow_hbm, wide_hbm, out_ref,
+    field_ref, narrow_ref, wide_ref, held, gain, turn, own_scale, scale_x, scale_y,
     outgoing, arrived, lines, returning, landed,
     small_sems, load_sem, send_sem, recv_sems, back_send_sem, back_recv_sems,
 ):
     me = lax.axis_index("cols")
     barrier = pltpu.get_barrier_semaphore()
+    left_ref, last_ref, right_ref = (narrow_ref.at[k * L : (k + 1) * L] for k in range(3))
+    lanes_ref, lanes_last_ref = (wide_ref.at[k * 256 : (k + 1) * 256] for k in range(2))
 
     def greet(k, carry):
         pl.semaphore_signal(
@@ -144,11 +146,8 @@
         for k, (source, target) in enumerate(
             [
                 (field_hbm, field_ref),
-                (left_hbm, left_ref),
-                (lanes_hbm, lanes_ref),
-                (last_hbm, last_ref),
-                (lanes_last_hbm, lanes_last_ref),
-                (right_hbm, right_ref),
+                (narrow_hbm, narrow_ref),
+                (wide_hbm, wide_ref),
             ]
         )
     ]
@@ -373,24 +372,20 @@
     columns = np.arange(128).reshape(2, HALVES, 32).transpose(1, 0, 2).reshape(128)
     forward = circulant(hop_rate)
     inverse = circulant(-hop_rate)
-    left = jnp.asarray(as_left(forward[np.ix_(order, order)]))
-    last = jnp.asarray(as_left(forward[:, order]))
-    lanes = jnp.asarray(as_right(forward, np.arange(128)))
-    lanes_last = jnp.asarray(as_right(forward, columns))
-    right = jnp.asarray(as_left(inverse))
+    narrow = np.concatenate(
+        [as_left(forward[np.ix_(order, order)]), as_left(forward[:, order]), as_left(inverse)], axis=0
+    )
+    wide = np.concatenate([as_right(forward, np.arange(128)), as_right(forward, columns)], axis=0)
     vmem = pl.BlockSpec(memory_space=pltpu.VMEM)
     wrapped = pl.pallas_call(
         kernel,
         out_shape=pltpu.VMEM((L, SITES), jnp.float32),
-        in_specs=[pl.BlockSpec(memory_space=pl.ANY)] * 7,
+        in_specs=[pl.BlockSpec(memory_space=pl.ANY)] * 4,
         out_specs=vmem,
         scratch_shapes=[
             pltpu.VMEM((SLICES * TILES, 128), jnp.int32),
-            pltpu.VMEM(left.shape, jnp.bfloat16),
-            pltpu.VMEM(last.shape, jnp.bfloat16),
-            pltpu.VMEM(lanes.shape, jnp.bfloat16),
-            pltpu.VMEM(lanes_last.shape, jnp.bfloat16),
-            pltpu.VMEM(right.shape, jnp.bfloat16),
+            pltpu.VMEM(narrow.shape, jnp.bfloat16),
+            pltpu.VMEM(wide.shape, jnp.bfloat16),
             pltpu.VMEM((TILES * PITCH_IN, 128), jnp.float32),
             pltpu.VMEM((SLICES * L, 128), jnp.float32),
             pltpu.VMEM((4 * L, 128), jnp.float32),
@@ -402,7 +397,7 @@
             pltpu.VMEM((ROWS * PITCH_X, 128), jnp.float32),
             pltpu.VMEM((HALVES * PEERS * PITCH_OUT, 128), jnp.float32),
             pltpu.VMEM((HALVES * PEERS, ROWS, 128), jnp.float32),
-            pltpu.SemaphoreType.DMA((6,)),
+            pltpu.SemaphoreType.DMA((3,)),
             pltpu.SemaphoreType.DMA,
             pltpu.SemaphoreType.DMA,
             pltpu.SemaphoreType.DMA((HALVES * ROWS // GROUP,)),
@@ -410,7 +405,7 @@
             pltpu.SemaphoreType.DMA((TILES // MERGED,)),
         ],
         compiler_params=pltpu.CompilerParams(collective_id=0, has_side_effects=True),
-    )(green, bits, left, last, lanes, lanes_last, right)
+    )(green, bits, jnp.asarray(narrow), jnp.asarray(wide))
     return wrapped.reshape(1, L, SITES)
 
 

time: 59 us -> 59.1 us (level)
  no operation moved by 1% of the time
where the time goes in v5:
time: 59.1 us; the launch traced here: 59 us
  Pallas kernels  58 us (98%)
  local copies, waits for them, and re-layouts  0.97 us (2%)
    pallas_call x1, Pallas kernels, shards(): pl.pallas_call(kernel, out_shape=pltpu.VMEM((L, SITES), jnp.float32), in_...  58 us

profile of v5, /device:TPU:2, one launch (start us, length us, event | category | flops | bytes accessed | tf_op | source)
XLA Modules:
  0.0 59.0 jit_solution(17240105961781321676)
XLA Ops:
  0.0 58.0 %shard_map.46 = f32[64,4096]{1,0:T(8,128)S(1)} custom-call(f32[64,4096]{1,0:T(8,128)} %bitcast.4, s32[96,128]{1,0:T(8,128)} %bitcast.5, bf16[192,192]{1,0:T(8,128)(2,1)} %constant.4.clone.narrow_hbm, bf16[512,256]{1,0:T(8,128)(2,1)} %constant.5.clone.wide_hbm), custom_call_target="tpu_custom_call" | custom-call | tf_op jit(solution)/shard_map/pallas_call | solution.py:380
  58.0 1.0 %copy.6 = f32[1,64,4096]{2,1,0:T(8,128)} copy(f32[1,64,4096]{2,1,0:T(8,128)S(1)} %bitcast.3) | data formatting | bytes 2097152

commit v6 on v3

--- a/solution.py
+++ b/solution.py
@@ -129,7 +129,8 @@
         )
         return carry
 
-    lax.fori_loop(1, PEERS, greet, 0)
+    for k in range(1, PEERS):
+        greet(k, 0)
 
     loads = [
         pltpu.make_async_copy(

time: 59 us -> 58.9 us (level)
  no operation moved by 1% of the time
where the time goes in v6:
time: 58.9 us; the launch traced here: 58.8 us
  Pallas kernels  57.8 us (98%)
  local copies, waits for them, and re-layouts  0.97 us (2%)
    pallas_call x1, Pallas kernels, shards(): pl.pallas_call(kernel, out_shape=pltpu.VMEM((L, SITES), jnp.float32), in_...  57.8 us

profile of v6, /device:TPU:2, one launch (start us, length us, event | category | flops | bytes accessed | tf_op | source)
XLA Modules:
  0.0 58.8 jit_solution(1800431272240109232)
XLA Ops:
  0.0 57.8 %shard_map.73 = f32[64,4096]{1,0:T(8,128)S(1)} custom-call(f32[64,4096]{1,0:T(8,128)} %bitcast.4, s32[96,128]{1,0:T(8,128)} %bitcast.5, bf16[64,192]{1,0:T(8,128)(2,1)} %constant.10.clone.left_hbm, bf16[64,192]{1,0:T(8,128)(2,1)} %constant.11.clone.last_hbm, bf16[256,256]{1,0:T(8,128)(2,1)} %constant.12.clone.lanes_hbm, ...), custom_call_target="tpu_custom_call" | custom-call | tf_op jit(solution)/shard_map/pallas_call | solution.py:383
  57.8 1.0 %copy.9 = f32[1,64,4096]{2,1,0:T(8,128)} copy(f32[1,64,4096]{2,1,0:T(8,128)S(1)} %bitcast.3) | data formatting | bytes 2097152
